TPU v7x, 32 devices: a whole 2x2x4 slice. The times are simulated.
32 devices in a mesh: rep: 2 (over x), gx: 16 (over z, y, core).
Axes of the slice: x: 2, y: 2, z: 4, core: 2. Of those that a mesh axis runs over, the one named last changes fastest.
Arguments:
- positions: float32 [3, 131072], P(None, ('rep', 'gx')), parts along dimension 1, may hold values from 0 to 128, as said below
- polar: float32 [131072], P(('rep', 'gx')), parts along dimension 0, may hold values from 0.25 to 1
- field_ext: float32 [3, 131072], P(None, ('rep', 'gx')), parts along dimension 1, may hold values from -10 to 10
- tile_atom: int32 [131072], P(('rep', 'gx')), parts along dimension 0, may hold values from 0 to 4095, as said below
- tile_list: int32 [1024, 3], P(('rep', 'gx')), parts along dimension 0, may hold values from 0 to 63, as said below
- image_shift: int32 [2, 1024, 3], P(None, ('rep', 'gx')), parts along dimension 1, may hold values from 0 to 1, as said below
Outputs:
- dipoles: float32 [3, 131072], P(None, ('rep', 'gx')), parts along dimension 1
- residual: float32 [3, 131072], P(None, ('rep', 'gx')), parts along dimension 1
There are 2 independent parts, one for each index of `rep`. A program takes and returns all parts, laid end to end along the dimension named above; each array names one. Nothing has to cross between parts.
Inputs may be any that keep to these rules, and one draw needn't show every extreme that they name: `positions`: coordinates lie in a box of 64 by 128 by 64; the atoms of slab s have first coordinate between 4 s and 4 s + 4; no two atoms, and no atom and a periodic image of another, are closer than 1.4. `tile_atom`: for each slab, a permutation of 0 to 4095. `tile_list`: entry 0 of a tile is the tile's own index within its slab. Entry n of a tile of slab s names tile n of slab s if n < 32, else tile n - 32 of slab s + 1 (slab 0 after the last). `image_shift`: offsets along the second and third coordinates in box lengths, one pair for each entry of tile_list; zero for entry 0.
All inputs are finite; a program needn't handle non-finite values.
Results may differ from a plain program's by a relative error of at most 0.0003.
Values sent between devices are 32-bit elements; how exact they have to be, the bound alone decides.
A program may use at most 64 MiB of HBM per device.

v0:
```python
import math

import jax
import jax.numpy as jnp
from jax import lax
from jax.sharding import PartitionSpec as P

ITERS = 4


thole_factor = 0.39


def passed_along(value, axis, steps):
    count = lax.axis_size(axis)
    pairs = [(source, (source + steps) % count) for source in range(count)]
    return lax.ppermute(value, axis, pairs)


def pair_block(
    place_left, root_left, moment_left, place_right, root_right, moment_right, weights, self_flags
):
    offset_x = place_right[:, 0, None, :] - place_left[:, 0, :, None]
    offset_y = place_right[:, 1, None, :] - place_left[:, 1, :, None]
    offset_z = place_right[:, 2, None, :] - place_left[:, 2, :, None]
    dist_sq = offset_x * offset_x + offset_y * offset_y + offset_z * offset_z
    tile_width = place_left.shape[2]
    row_ids = lax.broadcasted_iota(jnp.int32, (tile_width, tile_width), 0)
    column_ids = lax.broadcasted_iota(jnp.int32, (tile_width, tile_width), 1)
    same_atom = jnp.logical_and(self_flags[:, None, None] > 0, (row_ids == column_ids)[None])
    dist_sq = jnp.where(same_atom, 1.0, dist_sq)
    inv_dist = lax.rsqrt(dist_sq)
    distance = dist_sq * inv_dist
    damp_arg = thole_factor * dist_sq * distance / (root_left[:, :, None] * root_right[:, None, :])
    decay = jnp.exp(-damp_arg)
    inv_cube = jnp.where(same_atom, 0.0, weights[:, None, None] * inv_dist * inv_dist * inv_dist)
    coeff_three = (1.0 - decay) * inv_cube
    coeff_five = 3.0 * (1.0 - (1.0 + damp_arg) * decay) * inv_cube * inv_dist * inv_dist
    offsets = (offset_x, offset_y, offset_z)
    proj_right = (
        offset_x * moment_right[:, 0, None, :]
        + offset_y * moment_right[:, 1, None, :]
        + offset_z * moment_right[:, 2, None, :]
    )
    proj_left = (
        offset_x * moment_left[:, 0, :, None]
        + offset_y * moment_left[:, 1, :, None]
        + offset_z * moment_left[:, 2, :, None]
    )
    lift_right = coeff_five * proj_right
    lift_left = coeff_five * proj_left
    field_left = jnp.stack(
        [
            jnp.sum(
                lift_right * offsets[component] - coeff_three * moment_right[:, component, None, :],
                axis=2,
            )
            for component in range(3)
        ],
        axis=1,
    )
    field_right = jnp.stack(
        [
            jnp.sum(
                lift_left * offsets[component] - coeff_three * moment_left[:, component, :, None],
                axis=1,
            )
            for component in range(3)
        ],
        axis=1,
    )
    return (field_left, field_right)


def slab_fields(
    window_place,
    window_root,
    window_moment,
    left_index,
    right_index,
    image_vec,
    weights,
    self_flags,
):
    entries = left_index.shape[0]
    block_size = math.gcd(entries, 32)
    window_size = window_place.shape[0]
    tile_width = window_place.shape[2]
    slot_ids = jnp.arange(window_size, dtype=jnp.int32)

    def accumulate(summed, first_entry):
        left_rows = lax.dynamic_slice_in_dim(left_index, first_entry, block_size)
        right_rows = lax.dynamic_slice_in_dim(right_index, first_entry, block_size)
        image_rows = lax.dynamic_slice_in_dim(image_vec, first_entry, block_size)
        weight_rows = lax.dynamic_slice_in_dim(weights, first_entry, block_size)
        flag_rows = lax.dynamic_slice_in_dim(self_flags, first_entry, block_size)
        place_left = jnp.take(window_place, left_rows, axis=0)
        place_right = jnp.take(window_place, right_rows, axis=0) + image_rows[:, :, None]
        field_left, field_right = pair_block(
            place_left,
            jnp.take(window_root, left_rows, axis=0),
            jnp.take(window_moment, left_rows, axis=0),
            place_right,
            jnp.take(window_root, right_rows, axis=0),
            jnp.take(window_moment, right_rows, axis=0),
            weight_rows,
            flag_rows,
        )
        hit_left = (left_rows[:, None] == slot_ids[None, :]).astype(jnp.float32)
        hit_right = (right_rows[:, None] == slot_ids[None, :]).astype(jnp.float32)
        summed = summed + jnp.einsum(
            "ew,ef->wf",
            hit_left,
            field_left.reshape(block_size, 3 * tile_width),
            precision=lax.Precision.HIGHEST,
        )
        summed = summed + jnp.einsum(
            "ew,ef->wf",
            hit_right,
            field_right.reshape(block_size, 3 * tile_width),
            precision=lax.Precision.HIGHEST,
        )
        return (summed, None)

    first_entries = jnp.arange(0, entries, block_size, dtype=jnp.int32)
    summed, _ = lax.scan(
        accumulate, jnp.zeros((window_size, 3 * tile_width), jnp.float32), first_entries
    )
    return summed.reshape(window_size, 3, tile_width)


def image_vectors(lists, shifts, last_flag, tile_count, box_x, box_y, box_z):
    crossing = lists >= tile_count
    wrapped = jnp.where(jnp.logical_and(crossing, last_flag), box_x, 0.0)
    vectors = jnp.stack(
        [wrapped, shifts[0].astype(jnp.float32) * box_y, shifts[1].astype(jnp.float32) * box_z],
        axis=-1,
    )
    return vectors.reshape(-1, 3)


def two_products(vector, applied):
    return lax.psum((jnp.sum(vector * vector), jnp.sum(vector * applied)), "gx")


def on_device(positions, polar, field_ext, tile_atom, tile_list, image_shift):
    tile_count = tile_list.shape[0]
    links = tile_list.shape[1]
    atom_count = tile_atom.shape[0]
    tile_width = atom_count // tile_count
    slab_count = lax.axis_size("gx")
    position_id = lax.axis_index("gx")
    tiled_place = positions[:, tile_atom].reshape(3, tile_count, tile_width).transpose(1, 0, 2)
    tiled_polar = polar[tile_atom].reshape(tile_count, tile_width)
    tiled_root = jnp.sqrt(tiled_polar)
    tiled_rhs = field_ext[:, tile_atom].reshape(3, tile_count, tile_width).transpose(1, 0, 2)
    packed = jnp.concatenate([tiled_place, tiled_root[:, None, :]], axis=1)
    box_x = 4.0 * slab_count
    box_y = 128.0
    box_z = 2.0 * tile_count
    entry_ids = jnp.arange(links, dtype=jnp.int32)
    own_left = jnp.repeat(jnp.arange(tile_count, dtype=jnp.int32), links)
    own_right = tile_list.reshape(-1)
    own_weights = jnp.tile(jnp.where(entry_ids == 0, 0.5, 1.0), tile_count)
    own_self = jnp.tile((entry_ids == 0).astype(jnp.int32), tile_count)
    own_image = image_vectors(
        tile_list, image_shift, position_id == slab_count - 1, tile_count, box_x, box_y, box_z
    )
    ahead = passed_along(packed, "gx", -1)
    window_pack = jnp.concatenate([packed, ahead], axis=0)

    def operate(direction):
        ahead_moment = passed_along(direction, "gx", -1)
        summed = slab_fields(
            window_pack[:, :3],
            window_pack[:, 3],
            jnp.concatenate([direction, ahead_moment], axis=0),
            own_left,
            own_right,
            own_image,
            own_weights,
            own_self,
        )
        returned = passed_along(summed[tile_count:], "gx", 1)
        return direction / tiled_polar[:, None, :] - (summed[:tile_count] + returned)

    solution = jnp.zeros_like(tiled_rhs)
    resid = tiled_rhs
    applied = operate(resid)
    norm_now, product = two_products(resid, applied)
    step_size = norm_now / product
    direction, along = (resid, applied)
    for iteration in range(ITERS):
        solution = solution + step_size * direction
        resid = resid - step_size * along
        if iteration + 1 < ITERS:
            applied = operate(resid)
            norm_next, product = two_products(resid, applied)
            ratio = norm_next / norm_now
            step_size = norm_next / (product - ratio * norm_next / step_size)
            direction = resid + ratio * direction
            along = applied + ratio * along
            norm_now = norm_next
    dipoles = (
        jnp.zeros((3, atom_count), jnp.float32)
        .at[:, tile_atom]
        .set(solution.transpose(1, 0, 2).reshape(3, atom_count))
    )
    residual = (
        jnp.zeros((3, atom_count), jnp.float32)
        .at[:, tile_atom]
        .set(resid.transpose(1, 0, 2).reshape(3, atom_count))
    )
    return (dipoles, residual)


def solution(mesh):
    in_specs = (
        P(None, ("rep", "gx")),
        P(("rep", "gx")),
        P(None, ("rep", "gx")),
        P(("rep", "gx")),
        P(("rep", "gx"), None),
        P(None, ("rep", "gx"), None),
    )
    out_specs = (P(None, ("rep", "gx")), P(None, ("rep", "gx")))
    return jax.shard_map(
        on_device, mesh=mesh, in_specs=in_specs, out_specs=out_specs, check_vma=False
    )
```

profile of v0, /device:TPU:0, one launch (start us, length us, event | category | flops | bytes accessed | tf_op | source)
XLA Modules:
  0.0 454.0 jit_solution(3441594671451597137)
XLA Ops:
  0.6 0.7 broadcast_clamp_fusion
  1.4 23.0 %gather_fusion.25 = f32[4096]{0:T(1024)S(1)} fusion(f32[4096]{0:T(1024)S(1)} %copy-done, s32[4096]{0:T(1024)S(1)} %get-tuple-element.959), kind=kCustom, calls=%fused_computation.25 | custom fusion | bytes 49152 | tf_op jit(solution)/shard_map/gather | solution.py:154
  25.1 14.1 %gather_fusion.26 = f32[4096,3]{1,0:T(8,128)} fusion(f32[3,4096]{0,1:T(8,128)S(1)} %copy.89, s32[4096]{0:T(1024)S(1)} %get-tuple-element.959), kind=kCustom, calls=%fused_computation.26 | custom fusion | bytes 114688 | tf_op jit(solution)/shard_map/gather | solution.py:153
  39.2 2.2 copy.90
  41.4 5.5 %collective-permute-start = (f32[32,4,128]{2,0,1:T(8,128)S(1)}, f32[32,4,128]{2,0,1:T(8,128)S(1)}, u32[]{:S(2)}, u32[]{:S(2)}) collective-permute-start(f32[32,4,128]{2,0,1:T(8,128)S(1)} %pad_maximum_fusion.5), channel_id=1, source_target_pairs={{0,15},{1,0},{2,1},{3,2},{4,3},{5,4},{6,5},{7,6},{8,7},{9,8},{10,9... | collective-permute-start | bytes 196616 | tf_op jit(solution)/shard_map/ppermute | solution.py:17
  47.6 14.1 %gather_fusion.24 = f32[4096,3]{1,0:T(8,128)} fusion(f32[3,4096]{0,1:T(8,128)S(1)} %copy.86, s32[4096]{0:T(1024)S(1)} %get-tuple-element.959), kind=kCustom, calls=%fused_computation.24 | custom fusion | bytes 114688 | tf_op jit(solution)/shard_map/gather | solution.py:156
  61.7 2.2 copy.87
  63.9 0.7 collective-permute-start.1
  65.8 0.7 collective-permute-done.1
  66.7 46.8 %while.48 = (s32[]{:T(128)}, f32[64,384]{1,0:T(8,128)S(1)}, s32[3]{0:T(128)S(1)}, s32[96]{0:T(128)S(1)}, s32[96]{0:T(128)S(1)}, /*index=5*/s32[96]{0:T(128)S(1)}...) while((s32[]{:T(128)}, f32[64,384]{1,0:T(8,128)S(1)}, ...), condition=%wide.region_9.12_spmd.clone.clone, body=%wide.region_2.11_spmd.clone.clone.sunk | while | flops 53144164 | bytes 2176077 | solution.py:126
  73.9 7.8 %fusion.181 = (f32[32,128]{1,0:T(8,128)S(1)}, f32[32,128]{1,0:T(8,128)S(1)}, f32[32,128]{1,0:T(8,128)S(1)}, f32[32,128]{1,0:T(8,128)S(1)}, f32[32,128]{1,0:T(8,128)S(1)}, /*index=5*/f32[32,128]{1,0:T(8,128)S(1)}) fusion(f32[32,128]{1,0:T(8,128)S(1)} %bitcast.385, f32[32,128]{1,0:T(8,128)S(1)} %bitcast.397, f32[32,128]{1,0:T(8,128)S(1)} %bitcast.361, ...), kind=kLoop, calls=%fused_computation.66.clone.1 | loop fusion | flops 34054144 | bytes 344224 | tf_op jit(solution)/shard_map/while/body/eval_jaxpr/reduce_sum | solution.py:64
  89.5 7.8 %fusion.181 = (f32[32,128]{1,0:T(8,128)S(1)}, f32[32,128]{1,0:T(8,128)S(1)}, f32[32,128]{1,0:T(8,128)S(1)}, f32[32,128]{1,0:T(8,128)S(1)}, f32[32,128]{1,0:T(8,128)S(1)}, /*index=5*/f32[32,128]{1,0:T(8,128)S(1)}) fusion(f32[32,128]{1,0:T(8,128)S(1)} %bitcast.385, f32[32,128]{1,0:T(8,128)S(1)} %bitcast.397, f32[32,128]{1,0:T(8,128)S(1)} %bitcast.361, ...), kind=kLoop, calls=%fused_computation.66.clone.1 | loop fusion | flops 34054144 | bytes 344224 | tf_op jit(solution)/shard_map/while/body/eval_jaxpr/reduce_sum | solution.py:64
  105.1 7.8 %fusion.181 = (f32[32,128]{1,0:T(8,128)S(1)}, f32[32,128]{1,0:T(8,128)S(1)}, f32[32,128]{1,0:T(8,128)S(1)}, f32[32,128]{1,0:T(8,128)S(1)}, f32[32,128]{1,0:T(8,128)S(1)}, /*index=5*/f32[32,128]{1,0:T(8,128)S(1)}) fusion(f32[32,128]{1,0:T(8,128)S(1)} %bitcast.385, f32[32,128]{1,0:T(8,128)S(1)} %bitcast.397, f32[32,128]{1,0:T(8,128)S(1)} %bitcast.361, ...), kind=kLoop, calls=%fused_computation.66.clone.1 | loop fusion | flops 34054144 | bytes 344224 | tf_op jit(solution)/shard_map/while/body/eval_jaxpr/reduce_sum | solution.py:64
  113.7 6.4 %collective-permute-done.2 = f32[32,3,128]{2,1,0:T(4,128)S(1)} collective-permute-done((f32[32,3,128]{2,1,0:T(4,128)S(1)}, f32[32,3,128]{2,1,0:T(4,128)S(1)}, u32[]{:S(2)}, u32[]{:S(2)}) %collective-permute-start.2) | collective-permute-done | bytes 49184 | tf_op jit(solution)/shard_map/ppermute | solution.py:17
  120.7 30.1 %all-reduce.3 = (f32[]{:T(128)}, f32[]{:T(128)}) all-reduce(f32[]{:T(128)} %get-tuple-element.759, f32[]{:T(128)} %get-tuple-element.758), channel_id=1, replica_groups=mesh['rep'=2,'gx'=16] {'gx'}, use_global_device_ids=true, to_apply=%region_1.2 | all-reduce | flops 2 | bytes 16 | tf_op jit(solution)/shard_map/psum | solution.py:143
  152.3 1.9 collective-permute-done.3
  154.2 47.5 %while.49 = (s32[]{:T(128)}, f32[64,384]{1,0:T(8,128)S(1)}, s32[3]{0:T(128)S(1)}, s32[96]{0:T(128)S(1)}, s32[96]{0:T(128)S(1)}, /*index=5*/s32[96]{0:T(128)S(1)}...) while((s32[]{:T(128)}, f32[64,384]{1,0:T(8,128)S(1)}, ...), condition=%wide.region_21.24_spmd.clone.clone, body=%wide.region_14.23_spmd.clone.clone.sunk | while | flops 53144164 | bytes 2176077 | solution.py:126
  161.6 7.8 %fusion.188 = (f32[32,128]{1,0:T(8,128)S(1)}, f32[32,128]{1,0:T(8,128)S(1)}, f32[32,128]{1,0:T(8,128)S(1)}, f32[32,128]{1,0:T(8,128)S(1)}, f32[32,128]{1,0:T(8,128)S(1)}, /*index=5*/f32[32,128]{1,0:T(8,128)S(1)}) fusion(f32[32,128]{1,0:T(8,128)S(1)} %bitcast.388, f32[32,128]{1,0:T(8,128)S(1)} %bitcast.400, f32[32,128]{1,0:T(8,128)S(1)} %bitcast.364, ...), kind=kLoop, calls=%fused_computation.137.clone.1 | loop fusion | flops 34054144 | bytes 344224 | tf_op jit(solution)/shard_map/while/body/eval_jaxpr/reduce_sum | solution.py:64
  177.4 7.8 %fusion.188 = (f32[32,128]{1,0:T(8,128)S(1)}, f32[32,128]{1,0:T(8,128)S(1)}, f32[32,128]{1,0:T(8,128)S(1)}, f32[32,128]{1,0:T(8,128)S(1)}, f32[32,128]{1,0:T(8,128)S(1)}, /*index=5*/f32[32,128]{1,0:T(8,128)S(1)}) fusion(f32[32,128]{1,0:T(8,128)S(1)} %bitcast.388, f32[32,128]{1,0:T(8,128)S(1)} %bitcast.400, f32[32,128]{1,0:T(8,128)S(1)} %bitcast.364, ...), kind=kLoop, calls=%fused_computation.137.clone.1 | loop fusion | flops 34054144 | bytes 344224 | tf_op jit(solution)/shard_map/while/body/eval_jaxpr/reduce_sum | solution.py:64
  193.2 7.8 %fusion.188 = (f32[32,128]{1,0:T(8,128)S(1)}, f32[32,128]{1,0:T(8,128)S(1)}, f32[32,128]{1,0:T(8,128)S(1)}, f32[32,128]{1,0:T(8,128)S(1)}, f32[32,128]{1,0:T(8,128)S(1)}, /*index=5*/f32[32,128]{1,0:T(8,128)S(1)}) fusion(f32[32,128]{1,0:T(8,128)S(1)} %bitcast.388, f32[32,128]{1,0:T(8,128)S(1)} %bitcast.400, f32[32,128]{1,0:T(8,128)S(1)} %bitcast.364, ...), kind=kLoop, calls=%fused_computation.137.clone.1 | loop fusion | flops 34054144 | bytes 344224 | tf_op jit(solution)/shard_map/while/body/eval_jaxpr/reduce_sum | solution.py:64
  201.7 1.7 collective-permute-start.4
  203.4 4.8 %collective-permute-done.4 = f32[32,3,128]{2,1,0:T(4,128)S(1)} collective-permute-done((f32[32,3,128]{2,1,0:T(4,128)S(1)}, f32[32,3,128]{2,1,0:T(4,128)S(1)}, u32[]{:S(2)}, u32[]{:S(2)}) %collective-permute-start.4) | collective-permute-done | bytes 49184 | tf_op jit(solution)/shard_map/ppermute | solution.py:17
  208.2 0.7 multiply_reduce_fusion.4
  208.9 30.2 %all-reduce.2 = (f32[]{:T(128)}, f32[]{:T(128)}) all-reduce(f32[]{:T(128)} %get-tuple-element.757, f32[]{:T(128)} %get-tuple-element.756), channel_id=1, replica_groups=mesh['rep'=2,'gx'=16] {'gx'}, use_global_device_ids=true, to_apply=%region_13.16 | all-reduce | flops 2 | bytes 16 | tf_op jit(solution)/shard_map/psum | solution.py:143
  243.8 1.9 collective-permute-done.5
  245.7 46.8 %while.50 = (s32[]{:T(128)}, f32[64,384]{1,0:T(8,128)S(1)}, s32[3]{0:T(128)S(1)}, s32[96]{0:T(128)S(1)}, s32[96]{0:T(128)S(1)}, /*index=5*/s32[96]{0:T(128)S(1)}...) while((s32[]{:T(128)}, f32[64,384]{1,0:T(8,128)S(1)}, ...), condition=%wide.region_33.36_spmd.clone.clone, body=%wide.region_26.35_spmd.clone.clone.sunk | while | flops 53144164 | bytes 2176077 | solution.py:126
  252.9 7.8 %fusion.195 = (f32[32,128]{1,0:T(8,128)S(1)}, f32[32,128]{1,0:T(8,128)S(1)}, f32[32,128]{1,0:T(8,128)S(1)}, f32[32,128]{1,0:T(8,128)S(1)}, f32[32,128]{1,0:T(8,128)S(1)}, /*index=5*/f32[32,128]{1,0:T(8,128)S(1)}) fusion(f32[32,128]{1,0:T(8,128)S(1)} %bitcast.391, f32[32,128]{1,0:T(8,128)S(1)} %bitcast.403, f32[32,128]{1,0:T(8,128)S(1)} %bitcast.367, ...), kind=kLoop, calls=%fused_computation.208.clone.1 | loop fusion | flops 34054144 | bytes 344224 | tf_op jit(solution)/shard_map/while/body/eval_jaxpr/reduce_sum | solution.py:64
  268.5 7.8 %fusion.195 = (f32[32,128]{1,0:T(8,128)S(1)}, f32[32,128]{1,0:T(8,128)S(1)}, f32[32,128]{1,0:T(8,128)S(1)}, f32[32,128]{1,0:T(8,128)S(1)}, f32[32,128]{1,0:T(8,128)S(1)}, /*index=5*/f32[32,128]{1,0:T(8,128)S(1)}) fusion(f32[32,128]{1,0:T(8,128)S(1)} %bitcast.391, f32[32,128]{1,0:T(8,128)S(1)} %bitcast.403, f32[32,128]{1,0:T(8,128)S(1)} %bitcast.367, ...), kind=kLoop, calls=%fused_computation.208.clone.1 | loop fusion | flops 34054144 | bytes 344224 | tf_op jit(solution)/shard_map/while/body/eval_jaxpr/reduce_sum | solution.py:64
  284.1 7.8 %fusion.195 = (f32[32,128]{1,0:T(8,128)S(1)}, f32[32,128]{1,0:T(8,128)S(1)}, f32[32,128]{1,0:T(8,128)S(1)}, f32[32,128]{1,0:T(8,128)S(1)}, f32[32,128]{1,0:T(8,128)S(1)}, /*index=5*/f32[32,128]{1,0:T(8,128)S(1)}) fusion(f32[32,128]{1,0:T(8,128)S(1)} %bitcast.391, f32[32,128]{1,0:T(8,128)S(1)} %bitcast.403, f32[32,128]{1,0:T(8,128)S(1)} %bitcast.367, ...), kind=kLoop, calls=%fused_computation.208.clone.1 | loop fusion | flops 34054144 | bytes 344224 | tf_op jit(solution)/shard_map/while/body/eval_jaxpr/reduce_sum | solution.py:64
  292.6 1.7 collective-permute-start.6
  294.3 4.8 %collective-permute-done.6 = f32[32,3,128]{2,1,0:T(4,128)S(1)} collective-permute-done((f32[32,3,128]{2,1,0:T(4,128)S(1)}, f32[32,3,128]{2,1,0:T(4,128)S(1)}, u32[]{:S(2)}, u32[]{:S(2)}) %collective-permute-start.6) | collective-permute-done | bytes 49184 | tf_op jit(solution)/shard_map/ppermute | solution.py:17
  299.1 0.7 multiply_reduce_fusion.2
  299.7 30.1 %all-reduce.1 = (f32[]{:T(128)}, f32[]{:T(128)}) all-reduce(f32[]{:T(128)} %get-tuple-element.755, f32[]{:T(128)} %get-tuple-element.754), channel_id=1, replica_groups=mesh['rep'=2,'gx'=16] {'gx'}, use_global_device_ids=true, to_apply=%region_25.28 | all-reduce | flops 2 | bytes 16 | tf_op jit(solution)/shard_map/psum | solution.py:143
  334.1 1.9 collective-permute-done.7
  336.0 47.5 %while.51 = (s32[]{:T(128)}, f32[64,384]{1,0:T(8,128)S(1)}, s32[3]{0:T(128)S(1)}, s32[96]{0:T(128)S(1)}, s32[96]{0:T(128)S(1)}, /*index=5*/s32[96]{0:T(128)S(1)}...) while((s32[]{:T(128)}, f32[64,384]{1,0:T(8,128)S(1)}, ...), condition=%wide.region_45.48_spmd.clone.clone, body=%wide.region_38.47_spmd.clone.clone.sunk | while | flops 53144164 | bytes 2176077 | solution.py:126
  343.4 7.8 %fusion.202 = (f32[32,128]{1,0:T(8,128)S(1)}, f32[32,128]{1,0:T(8,128)S(1)}, f32[32,128]{1,0:T(8,128)S(1)}, f32[32,128]{1,0:T(8,128)S(1)}, f32[32,128]{1,0:T(8,128)S(1)}, /*index=5*/f32[32,128]{1,0:T(8,128)S(1)}) fusion(f32[32,128]{1,0:T(8,128)S(1)} %bitcast.394, f32[32,128]{1,0:T(8,128)S(1)} %bitcast.406, f32[32,128]{1,0:T(8,128)S(1)} %bitcast.370, ...), kind=kLoop, calls=%fused_computation.279.clone.1 | loop fusion | flops 34054144 | bytes 344224 | tf_op jit(solution)/shard_map/while/body/eval_jaxpr/reduce_sum | solution.py:64
  359.2 7.8 %fusion.202 = (f32[32,128]{1,0:T(8,128)S(1)}, f32[32,128]{1,0:T(8,128)S(1)}, f32[32,128]{1,0:T(8,128)S(1)}, f32[32,128]{1,0:T(8,128)S(1)}, f32[32,128]{1,0:T(8,128)S(1)}, /*index=5*/f32[32,128]{1,0:T(8,128)S(1)}) fusion(f32[32,128]{1,0:T(8,128)S(1)} %bitcast.394, f32[32,128]{1,0:T(8,128)S(1)} %bitcast.406, f32[32,128]{1,0:T(8,128)S(1)} %bitcast.370, ...), kind=kLoop, calls=%fused_computation.279.clone.1 | loop fusion | flops 34054144 | bytes 344224 | tf_op jit(solution)/shard_map/while/body/eval_jaxpr/reduce_sum | solution.py:64
  375.0 7.8 %fusion.202 = (f32[32,128]{1,0:T(8,128)S(1)}, f32[32,128]{1,0:T(8,128)S(1)}, f32[32,128]{1,0:T(8,128)S(1)}, f32[32,128]{1,0:T(8,128)S(1)}, f32[32,128]{1,0:T(8,128)S(1)}, /*index=5*/f32[32,128]{1,0:T(8,128)S(1)}) fusion(f32[32,128]{1,0:T(8,128)S(1)} %bitcast.394, f32[32,128]{1,0:T(8,128)S(1)} %bitcast.406, f32[32,128]{1,0:T(8,128)S(1)} %bitcast.370, ...), kind=kLoop, calls=%fused_computation.279.clone.1 | loop fusion | flops 34054144 | bytes 344224 | tf_op jit(solution)/shard_map/while/body/eval_jaxpr/reduce_sum | solution.py:64
  383.5 1.7 collective-permute-start.8
  385.2 4.8 %collective-permute-done.8 = f32[32,3,128]{2,1,0:T(4,128)S(1)} collective-permute-done((f32[32,3,128]{2,1,0:T(4,128)S(1)}, f32[32,3,128]{2,1,0:T(4,128)S(1)}, u32[]{:S(2)}, u32[]{:S(2)}) %collective-permute-start.8) | collective-permute-done | bytes 49184 | tf_op jit(solution)/shard_map/ppermute | solution.py:17
  390.0 0.7 multiply_reduce_fusion
  390.7 30.1 %all-reduce = (f32[]{:T(128)}, f32[]{:T(128)}) all-reduce(f32[]{:T(128)} %get-tuple-element.753, f32[]{:T(128)} %get-tuple-element.752), channel_id=1, replica_groups=mesh['rep'=2,'gx'=16] {'gx'}, use_global_device_ids=true, to_apply=%region_37.40 | all-reduce | flops 2 | bytes 16 | tf_op jit(solution)/shard_map/psum | solution.py:143
  424.7 2.0 copy.101
  426.7 11.4 %scatter_custom_fusion.1 = f32[3,4096]{0,1:T(8,128)S(1)} fusion(s32[4096]{0:T(1024)S(1)} %get-tuple-element.960, f32[4096,3]{1,0:T(8,128)} %copy.101, f32[]{:T(128)} %constant.17.clone.1), kind=kCustom, calls=%fused_computation.317 | custom fusion | bytes 49664 | tf_op jit(solution)/shard_map/scatter | solution.py:212
  438.1 1.2 copy.103
  439.3 2.0 copy.100
  441.3 11.4 %scatter_custom_fusion = f32[3,4096]{0,1:T(8,128)S(1)} fusion(s32[4096]{0:T(1024)S(1)} %get-tuple-element.960, f32[4096,3]{1,0:T(8,128)} %copy.100, f32[]{:T(128)} %constant.17.clone.1), kind=kCustom, calls=%fused_computation.319 | custom fusion | bytes 49664 | tf_op jit(solution)/shard_map/scatter | solution.py:207
  452.8 1.2 copy.102
  (393 shorter events, 73.7 us)
Async XLA Ops:
  0.6 0.7 copy-start
  1.4 23.1 %copy-start.1 = (f32[3,4096]{1,0:T(4,128)S(1)}, f32[3,4096]{1,0:T(4,128)}, u32[]{:S(2)}) copy-start(f32[3,4096]{1,0:T(4,128)} %param.18) | copy-start | bytes 147460
  24.5 22.5 %copy-start.2 = (f32[3,4096]{1,0:T(4,128)S(1)}, f32[3,4096]{1,0:T(4,128)}, u32[]{:S(2)}) copy-start(f32[3,4096]{1,0:T(4,128)} %param.20) | copy-start | bytes 147460
  41.4 23.2 %copy-start.4 = (s32[2,32,3]{1,0,2:T(2,128)S(1)}, s32[2,32,3]{1,0,2:T(2,128)}, u32[]{:S(2)}) copy-start(s32[2,32,3]{1,0,2:T(2,128)} %param.23) | copy-start | bytes 2308
  41.4 23.6 %copy-start.3 = (s32[32,3]{0,1:T(4,128)S(1)}, s32[32,3]{0,1:T(4,128)}, u32[]{:S(2)}) copy-start(s32[32,3]{0,1:T(4,128)} %param.22) | copy-start | bytes 1156
  41.4 25.1 %collective-permute-start = (f32[32,4,128]{2,0,1:T(8,128)S(1)}, f32[32,4,128]{2,0,1:T(8,128)S(1)}, u32[]{:S(2)}, u32[]{:S(2)}) collective-permute-start(f32[32,4,128]{2,0,1:T(8,128)S(1)} %pad_maximum_fusion.5), channel_id=1, source_target_pairs={{0,15},{1,0},{2,1},{3,2},{4,3},{5,4},{6,5},{7,6},{8,7},{9,8},{10,9... | collective-permute-start | bytes 196616 | tf_op jit(solution)/shard_map/ppermute | solution.py:17
  63.9 2.6 collective-permute-start.1
  113.6 6.5 %collective-permute-start.2 = (f32[32,3,128]{2,1,0:T(4,128)S(1)}, f32[32,3,128]{2,1,0:T(4,128)S(1)}, u32[]{:S(2)}, u32[]{:S(2)}) collective-permute-start(f32[32,3,128]{2,1,0:T(4,128)S(1)} %slice.241), channel_id=1, source_target_pairs={{0,1},{1,2},{2,3},{3,4},{4,5},{5,6},{6,7},{7,8},{8,9},{9,10},{10,1... | collective-permute-start | bytes 147464 | tf_op jit(solution)/shard_map/ppermute | solution.py:17
  152.2 2.0 collective-permute-start.3
  201.7 6.5 %collective-permute-start.4 = (f32[32,3,128]{2,1,0:T(4,128)S(1)}, f32[32,3,128]{2,1,0:T(4,128)S(1)}, u32[]{:S(2)}, u32[]{:S(2)}) collective-permute-start(f32[32,3,128]{2,1,0:T(4,128)S(1)} %slice.245), channel_id=1, source_target_pairs={{0,1},{1,2},{2,3},{3,4},{4,5},{5,6},{6,7},{7,8},{8,9},{9,10},{10,1... | collective-permute-start | bytes 147464 | tf_op jit(solution)/shard_map/ppermute | solution.py:17
  243.7 2.0 collective-permute-start.5
  292.6 6.5 %collective-permute-start.6 = (f32[32,3,128]{2,1,0:T(4,128)S(1)}, f32[32,3,128]{2,1,0:T(4,128)S(1)}, u32[]{:S(2)}, u32[]{:S(2)}) collective-permute-start(f32[32,3,128]{2,1,0:T(4,128)S(1)} %slice.249), channel_id=1, source_target_pairs={{0,1},{1,2},{2,3},{3,4},{4,5},{5,6},{6,7},{7,8},{8,9},{9,10},{10,1... | collective-permute-start | bytes 147464 | tf_op jit(solution)/shard_map/ppermute | solution.py:17
  333.8 2.1 collective-permute-start.7
  383.5 6.5 %collective-permute-start.8 = (f32[32,3,128]{2,1,0:T(4,128)S(1)}, f32[32,3,128]{2,1,0:T(4,128)S(1)}, u32[]{:S(2)}, u32[]{:S(2)}) collective-permute-start(f32[32,3,128]{2,1,0:T(4,128)S(1)} %slice.253), channel_id=1, source_target_pairs={{0,1},{1,2},{2,3},{3,4},{4,5},{5,6},{6,7},{7,8},{8,9},{9,10},{10,1... | collective-permute-start | bytes 147464 | tf_op jit(solution)/shard_map/ppermute | solution.py:17
where the time goes:
time: 455 us; the launch traced here: 454 us
  local copies, waits for them, and re-layouts  143 us (31%)
  blocking collectives  120 us (26%)
  other arithmetic  104 us (23%)
  waiting for transfers between devices  27 us (6%)
  loops' own time  25.6 us (6%)
  between operations  14.6 us (3%)
  starting transfers between devices  11.7 us (3%)
  matrix products  7.52 us (2%)
    psum x4, blocking collectives, two_products(): return lax.psum((jnp.sum(vector * vector), jnp.sum(vector * applied)), 'gx')  120 us
    reduce_sum x12, other arithmetic, pair_block(): jnp.sum(lift_left * offsets[component] - coeff_three * moment_left[:, com...  93.5 us
    ppermute x9, waiting for transfers between devices, passed_along(): return lax.ppermute(value, axis, pairs)  27 us
    another operation x4, loops' own time, slab_fields(): lax.scan(accumulate, jnp.zeros((window_size, 3 * tile_width), jnp.float32...  25.6 us
    gather x1, local copies, waits for them, and re-layouts, on_device(): tiled_polar = polar[tile_atom].reshape(tile_count, tile_width)  23 us
    gather x1, local copies, waits for them, and re-layouts, on_device(): positions[:, tile_atom].reshape(3, tile_count, tile_width)  14.1 us
    gather x1, local copies, waits for them, and re-layouts, on_device(): field_ext[:, tile_atom].reshape(3, tile_count, tile_width)  14.1 us
    ppermute x9, starting transfers between devices, passed_along(): return lax.ppermute(value, axis, pairs)  11.7 us
  transfers between devices with their start and end apart: 9, of which 8 were waited for; matrix products, arithmetic and copies ran while one was open for 4% of the time, Pallas kernels for 0%

commit v1 on v0

v1 whole, which is shorter than its diff:
```python
import functools

import jax
import jax.numpy as jnp
from jax import lax
from jax.experimental import pallas as pl
from jax.experimental.pallas import tpu as pltpu
from jax.sharding import PartitionSpec as P

ITERS = 4
MESH = pl.DeviceIdType.MESH
thole_factor = 0.39
ROWS = 16
F32 = jnp.float32
BF16 = jnp.bfloat16


def split_two(value):
    high = value.astype(BF16)
    return high, (value - high.astype(F32)).astype(BF16)


def split_three(value):
    high = value.astype(BF16)
    rest = value - high.astype(F32)
    middle = rest.astype(BF16)
    return high, middle, (rest - middle.astype(F32)).astype(BF16)


def gather_tile(row, source, tiles):
    width = 128
    inner = jnp.broadcast_to(row & (width - 1), (8, width))
    outer = jnp.broadcast_to(row >> 7, (8, width))
    value = jnp.zeros((8, width), F32)
    for tile in range(tiles):
        picked = jnp.take_along_axis(
            source[pl.ds(tile * 8, 8), :], inner, axis=1, mode="promise_in_bounds"
        )
        value = jnp.where(outer == tile, picked, value)
    return value


def tiling_kernel(
    tiles,
    links,
    list_ref,
    shift_ref,
    place_ref,
    polar_ref,
    field_ref,
    atom_ref,
    out_ref,
    inverse,
    hits,
    image,
    feat,
):
    width = 128
    near = links - 1
    for tile in range(tiles):
        lanes = pl.ds(tile * width, width)
        feat[tile * 8 : tile * 8 + 3, :] = place_ref[:, lanes]
        feat[tile * 8 + 3 : tile * 8 + 6, :] = field_ref[:, lanes]
        feat[tile * 8 + 6 : tile * 8 + 7, :] = polar_ref[:, lanes]
        feat[tile * 8 + 7 : tile * 8 + 8, :] = jnp.ones((1, width), F32)
    sub_ids = lax.broadcasted_iota(jnp.int32, (8, width), 0)

    def fill(tile, carry):
        value = gather_tile(atom_ref[pl.ds(tile, 1), :], feat, tiles)
        root = lax.rsqrt(value)
        value = jnp.where(sub_ids == 7, pltpu.roll(root, 1, 0), value)
        out_ref[pl.ds(pl.multiple_of(tile * 8, 8), 8), :] = value
        return carry

    lax.fori_loop(0, tiles, fill, 0)

    lane_ids = lax.broadcasted_iota(jnp.int32, (width, width), 0)
    tile_ids = lax.broadcasted_iota(jnp.int32, (tiles, width), 0)
    lane_row = lax.broadcasted_iota(jnp.int32, (tiles, width), 1).astype(F32)

    def invert(tile, total):
        row = atom_ref[pl.ds(tile, 1), :]
        outer = tile_ids == (row >> 7)
        number = jnp.full((tiles, width), tile, jnp.int32).astype(F32)
        left = jnp.concatenate(
            [jnp.where(outer, number, 0.0), jnp.where(outer, lane_row, 0.0)], axis=0
        ).astype(BF16)
        right = jnp.where(lane_ids == (row & (width - 1)), 1.0, 0.0).astype(BF16)
        return total + lax.dot_general(
            left, right, (((1,), (1,)), ((), ())), preferred_element_type=F32
        )

    found = lax.fori_loop(0, tiles, invert, jnp.zeros((2 * tiles, width), F32))
    inverse[...] = (found[:tiles] * float(width) + found[tiles:]).astype(jnp.int32)

    lane_one = lax.broadcasted_iota(jnp.int32, (1, width), 1)

    def name(tile, carry):
        for entry in range(near):
            slot = entry * tiles + tile
            named = list_ref[tile * links + entry + 1]
            hit = jnp.where((lane_one == named) | (lane_one == named + 2 * tiles), 1.0, 0.0)
            hits[pl.ds(slot, 1), :] = hit
            hits[pl.ds(near * tiles + slot, 1), :] = hit
            ones = jnp.ones((1, width), F32)
            crossing = jnp.where(named >= tiles, 1.0, 0.0)
            step_y = shift_ref[tile * links + entry + 1].astype(F32)
            step_z = shift_ref[(tiles + tile) * links + entry + 1].astype(F32)
            image[0, pl.ds(slot, 1), :] = ones * crossing
            image[1, pl.ds(slot, 1), :] = ones * step_y
            image[2, pl.ds(slot, 1), :] = ones * step_z
        return carry

    lax.fori_loop(0, tiles, name, 0)


def untiling_kernel(tiles, tiled_ref, inverse, dip_ref, res_ref):
    width = 128

    def give(tile, carry):
        value = gather_tile(inverse[pl.ds(tile, 1), :], tiled_ref, tiles)
        lanes = pl.ds(pl.multiple_of(tile * width, width), width)
        dip_ref[:, lanes] = value[0:3]
        res_ref[:, lanes] = value[3:6]
        return carry

    lax.fori_loop(0, tiles, give, 0)


def kernel(
    count,
    tiles,
    links,
    tiled_ref,
    hits_ref,
    image_ref,
    out_ref,
    window,
    pair_own,
    pair_back,
    pair_left,
    three_t,
    five_t,
    there,
    local,
    local_far,
    shift_left,
    shift_right,
    moments,
    minus,
    results,
    sent_w,
    ahead_w,
    sent_f,
    back_f,
    dots,
    pack_sem,
    w_sem,
    f_sem,
    dot_sem,
):
    width = 128
    near = links - 1
    me = lax.axis_index("gx")
    after = lax.rem(me + 1, count)
    before = lax.rem(me + count - 1, count)

    barrier = pltpu.get_barrier_semaphore()

    def greet(step, carry):
        pl.semaphore_signal(
            barrier, inc=1, device_id={"gx": lax.rem(me + step, count)}, device_id_type=MESH
        )
        return carry

    lax.fori_loop(1, count, greet, 0)

    sub_ids = lax.broadcasted_iota(jnp.int32, (8, width), 0)

    window[0 : tiles * 8, :] = tiled_ref[...]
    pl.semaphore_wait(barrier, count - 1)
    pack_copy = pltpu.make_async_remote_copy(
        src_ref=tiled_ref,
        dst_ref=window.at[pl.ds(tiles * 8, tiles * 8)],
        send_sem=pack_sem.at[0],
        recv_sem=pack_sem.at[1],
        device_id={"gx": before},
        device_id_type=MESH,
    )
    pack_copy.start()

    row_ids = lax.broadcasted_iota(jnp.int32, (16, width), 0)
    column_ids = lax.broadcasted_iota(jnp.int32, (16, width), 1)

    def pair_rows(columns, other, first, same):
        rows = slice(first, first + 16)
        off_x = other[0:1, :] - columns[rows, 0:1]
        off_y = other[1:2, :] - columns[rows, 1:2]
        off_z = other[2:3, :] - columns[rows, 2:3]
        dist_sq = off_x * off_x + off_y * off_y + off_z * off_z
        if same:
            mask = row_ids + first == column_ids
            dist_sq = jnp.where(mask, 1.0, dist_sq)
        inv = lax.rsqrt(dist_sq)
        inv_sq = inv * inv
        damp = dist_sq * dist_sq * inv * (columns[rows, 7:8] * (thole_factor * other[7:8, :]))
        decay = jnp.exp(-damp)
        inv_cube = inv * inv_sq
        if same:
            inv_cube = jnp.where(mask, 0.0, inv_cube)
        less = 1.0 - decay
        three = less * inv_cube
        five = 3.0 * (less - damp * decay) * (inv_cube * inv_sq)
        return three, five

    def store_pair(target, index, first, three, five):
        rows = slice(first, first + 16)
        more = slice(width + first, width + first + 16)
        high, low = split_two(five)
        target[index, rows, 0:width] = high
        target[index, rows, width : 2 * width] = low
        high, low = split_two(three)
        target[index, more, 0:width] = high
        target[index, more, width : 2 * width] = low

    def own_pairs(tile, carry):
        here = window[pl.ds(pl.multiple_of(tile * 8, 8), 8), :]
        columns = here.T
        for first in range(0, width, 16):
            three, five = pair_rows(columns, here, first, True)
            store_pair(pair_own, tile, first, three, five)
        return carry

    lax.fori_loop(0, tiles, own_pairs, 0)

    pack_copy.wait_recv()

    slots = near * tiles
    hit_own = hits_ref[0:slots, :].astype(BF16)
    hit_rows = hits_ref[...].T[0 : 2 * tiles].astype(BF16)

    def picked(matrix, values):
        high, middle, low = split_three(jnp.concatenate(values, axis=1))
        found = jnp.dot(
            matrix, jnp.concatenate([high, middle], axis=0), preferred_element_type=F32
        ) + jnp.dot(
            matrix,
            jnp.concatenate([low, jnp.zeros_like(low)], axis=0),
            preferred_element_type=F32,
        )
        return [found[:, part * width : (part + 1) * width] for part in range(len(values))]

    def middle_of(value):
        return jnp.floor(jnp.mean(value, axis=1, keepdims=True) + 0.5)

    both = [window[pl.ds(row, 2 * tiles, stride=8), :] for row in (0, 1, 2, 7)]
    named = picked(hit_own, both)
    there[pl.ds(7, slots, stride=8), :] = named[3]
    lengths = (jnp.where(me == count - 1, 4.0 * count, 0.0), 128.0, 2.0 * tiles)
    for axis in range(3):
        here = both[axis][0:tiles]
        here_middle = middle_of(here)
        local[axis] = here - here_middle
        far_middle = middle_of(named[axis])
        local_far[axis] = named[axis] - far_middle
        vector = image_ref[axis] * lengths[axis]
        moved = named[axis] + vector
        there[pl.ds(axis, slots, stride=8), :] = moved
        for entry in range(near):
            part = slice(entry * tiles, (entry + 1) * tiles)
            shift_left[axis, part, :] = here - (far_middle[part] + vector[part])
            shift_right[axis, part, :] = moved[part] - here_middle

    def far_pairs(tile, carry):
        here_rows = pl.ds(pl.multiple_of(tile * 8, 8), 8)
        here = window[here_rows, :]
        columns = here.T
        for entry in range(near):
            slot = entry * tiles + tile
            other = there[pl.ds(pl.multiple_of(slot * 8, 8), 8), :]
            for first in range(0, width, 16):
                three, five = pair_rows(columns, other, first, False)
                store_pair(pair_back, slot, first, three, five)
                three_t[entry, first : first + 16, :] = three
                five_t[entry, first : first + 16, :] = five
            three = three_t[entry].T
            five = five_t[entry].T
            for first in range(0, width, 16):
                store_pair(
                    pair_left, slot, first, three[first : first + 16], five[first : first + 16]
                )
        return carry

    lax.fori_loop(0, tiles, far_pairs, 0)
    minus[...] = jnp.zeros_like(minus)

    def build(vec, base_ref, size):
        base = [base_ref[axis] for axis in range(3)]
        along = base[0] * vec[0] + base[1] * vec[1] + base[2] * vec[2]

        def put(ref, row, value):
            ref[pl.ds(row, size, stride=ROWS), :] = value

        for axis in range(3):
            put(moments, axis, base[axis] * along)
            put(minus, axis, -vec[axis])
            for other in range(3):
                put(moments, 4 + 4 * axis + other, base[other] * vec[axis])
            put(moments, 7 + 4 * axis, vec[axis])
        put(moments, 3, along)

    def block_of(tile):
        rows = pl.ds(pl.multiple_of(tile * ROWS, ROWS), ROWS)
        return jnp.concatenate(
            [
                jnp.concatenate(split_three(moments[rows, :]), axis=0),
                jnp.concatenate(split_three(minus[rows, :]), axis=0),
            ],
            axis=1,
        )

    def product(block, weights, slot):
        out = jnp.dot(block, weights, preferred_element_type=F32)
        out = out[:, :width] + out[:, width:]
        results[pl.ds(pl.multiple_of(slot * ROWS, ROWS), ROWS), :] = (
            out[0:ROWS] + out[ROWS : 2 * ROWS]
        ) + out[2 * ROWS : 3 * ROWS]

    def combined(kind, shifts):
        def get(row):
            return results[pl.ds(kind * tiles * ROWS + row, tiles, stride=ROWS), :]

        parts = []
        for row in range(4):
            total = get(row)
            for axis in range(3):
                total = total - shifts[axis] * get(4 + 4 * axis + row)
            parts.append(total)
        return [parts[axis] - shifts[axis] * parts[3] for axis in range(3)]

    def shifts_of(ref, entry):
        return [ref[axis, entry * tiles : (entry + 1) * tiles, :] for axis in range(3)]

    alpha_inv = 1.0 / window[pl.ds(6, tiles, stride=8), :]

    def copy_w(turn):
        return pltpu.make_async_remote_copy(
            src_ref=sent_w.at[turn],
            dst_ref=ahead_w.at[turn],
            send_sem=w_sem.at[0, turn],
            recv_sem=w_sem.at[1, turn],
            device_id={"gx": before},
            device_id_type=MESH,
        )

    def copy_f(turn):
        return pltpu.make_async_remote_copy(
            src_ref=sent_f.at[turn],
            dst_ref=back_f.at[turn],
            send_sem=f_sem.at[0, turn],
            recv_sem=f_sem.at[1, turn],
            device_id={"gx": after},
            device_id_type=MESH,
        )

    def back_step(group, carry):
        for offset in range(4):
            tile = group * 4 + offset
            block = block_of(tile)
            product(block, pair_own[tile], tile)
            for entry in range(near):
                slot = entry * tiles + tile
                product(block, pair_back[slot], tiles + slot)
        return carry

    def left_step(group, carry):
        for offset in range(4):
            tile = group * 4 + offset
            for entry in range(near):
                slot = entry * tiles + tile
                product(block_of(slot), pair_left[slot], tiles + slot)
        return carry

    def applied(turn, vec):
        build(vec, local, tiles)
        lax.fori_loop(0, tiles // 4, back_step, 0)
        back = [combined(1 + entry, shifts_of(shift_right, entry)) for entry in range(near)]
        spread = picked(
            hit_rows,
            [
                jnp.concatenate([back[entry][axis] for entry in range(near)], axis=0)
                for axis in range(3)
            ],
        )
        for axis in range(3):
            sent_f[turn, axis] = spread[axis][tiles:]
        copy_f(turn).start()
        field = combined(0, [local[axis] for axis in range(3)])
        field = [field[axis] + spread[axis][:tiles] for axis in range(3)]
        if turn == 0:
            ahead = [window[pl.ds(tiles * 8 + 3 + axis, tiles, stride=8), :] for axis in range(3)]
        else:
            copy_w(turn).wait_recv()
            ahead = [ahead_w[turn, axis] for axis in range(3)]
        window_vec = [jnp.concatenate([vec[axis], ahead[axis]], axis=0) for axis in range(3)]
        build(picked(hit_own, window_vec), local_far, slots)
        lax.fori_loop(0, tiles // 4, left_step, 0)
        for entry in range(near):
            more = combined(1 + entry, shifts_of(shift_left, entry))
            field = [field[axis] + more[axis] for axis in range(3)]
        copy_f(turn).wait_recv()
        return [vec[axis] * alpha_inv - (field[axis] + back_f[turn, axis]) for axis in range(3)]

    def dot_rows(left, right):
        total = left[0] * right[0] + left[1] * right[1] + left[2] * right[2]
        return jnp.sum(total, axis=0, keepdims=True)

    def send_dots(turn, resid, w):
        dots[turn, 0] = jnp.where(
            sub_ids == 0, dot_rows(resid, resid), jnp.where(sub_ids == 1, dot_rows(resid, w), 0.0)
        )

        def send(step, carry):
            pltpu.make_async_remote_copy(
                src_ref=dots.at[turn, 0],
                dst_ref=dots.at[turn, step],
                send_sem=dot_sem.at[0, turn],
                recv_sem=dot_sem.at[1, turn],
                device_id={"gx": lax.rem(me + step, count)},
                device_id_type=MESH,
            ).start()
            return carry

        lax.fori_loop(1, count, send, 0)

    def wait_dots(turn, which):
        whole = dots.at[turn, pl.ds(1, count - 1)]
        pltpu.make_async_copy(whole, whole, dot_sem.at[which, turn]).wait()

    resid = [window[pl.ds(3 + axis, tiles, stride=8), :] for axis in range(3)]
    w = applied(0, resid)
    solution = direction = s = z = None
    norm_last = step_last = None
    for turn in range(ITERS):
        more_turns = turn + 1 < ITERS
        if more_turns:
            for axis in range(3):
                sent_w[turn + 1, axis] = w[axis]
            copy_w(turn + 1).start()
        send_dots(turn, resid, w)
        if more_turns:
            q = applied(turn + 1, w)
        wait_dots(turn, 1)
        sums = jnp.sum(jnp.sum(dots[turn], axis=0), axis=1, keepdims=True)
        norm = sums[0:1, :]
        product_now = sums[1:2, :]
        if turn == 0:
            step = norm / product_now
            direction, s = resid, w
            solution = [step * direction[axis] for axis in range(3)]
            if more_turns:
                z = q
        else:
            ratio = norm / norm_last
            step = norm / (product_now - ratio * norm / step_last)
            direction = [resid[axis] + ratio * direction[axis] for axis in range(3)]
            s = [w[axis] + ratio * s[axis] for axis in range(3)]
            solution = [solution[axis] + step * direction[axis] for axis in range(3)]
            if more_turns:
                z = [q[axis] + ratio * z[axis] for axis in range(3)]
        resid = [resid[axis] - step * s[axis] for axis in range(3)]
        if more_turns:
            w = [w[axis] - step * z[axis] for axis in range(3)]
        norm_last, step_last = norm, step

    def put_final(row, value):
        out_ref[pl.ds(row, tiles, stride=8), :] = value

    for axis in range(3):
        put_final(axis, solution[axis])
        put_final(3 + axis, resid[axis])
    put_final(6, jnp.zeros((tiles, width), F32))
    put_final(7, jnp.zeros((tiles, width), F32))

    pack_copy.wait_send()
    for turn in range(ITERS):
        if turn > 0:
            copy_w(turn).wait_send()
        copy_f(turn).wait_send()
        wait_dots(turn, 0)


def on_device(positions, polar, field_ext, tile_atom, tile_list, image_shift):
    tiles, links = tile_list.shape
    atoms = tile_atom.shape[0]
    width = atoms // tiles
    near = links - 1
    count = lax.axis_size("gx")
    pairs = (2 * width, 2 * width)
    vmem = pl.BlockSpec(memory_space=pltpu.VMEM)
    smem = pl.BlockSpec(memory_space=pltpu.SMEM)
    out = jax.ShapeDtypeStruct((3, atoms), F32)
    vectors = pltpu.VMEM((ITERS, 3, tiles, width), F32)
    tiled = jax.ShapeDtypeStruct((tiles * 8, width), F32)
    window, inverse, hits, image = pl.pallas_call(
        functools.partial(tiling_kernel, tiles, links),
        out_shape=(
            tiled,
            jax.ShapeDtypeStruct((tiles, width), jnp.int32),
            jax.ShapeDtypeStruct((2 * near * tiles, width), F32),
            jax.ShapeDtypeStruct((3, near * tiles, width), F32),
        ),
        in_specs=[smem, smem, vmem, vmem, vmem, vmem],
        out_specs=(vmem, vmem, vmem, vmem),
        scratch_shapes=[pltpu.VMEM((tiles * 8, width), F32)],
    )(
        tile_list.reshape(-1),
        image_shift.reshape(-1),
        positions,
        polar.reshape(1, atoms),
        field_ext,
        tile_atom.reshape(tiles, width),
    )
    found = pl.pallas_call(
        functools.partial(kernel, count, tiles, links),
        out_shape=tiled,
        in_specs=[vmem, vmem, vmem],
        out_specs=vmem,
        scratch_shapes=[
            pltpu.VMEM((2 * tiles * 8, width), F32),
            pltpu.VMEM((tiles,) + pairs, BF16),
            pltpu.VMEM((near * tiles,) + pairs, BF16),
            pltpu.VMEM((near * tiles,) + pairs, BF16),
            pltpu.VMEM((near, width, width), F32),
            pltpu.VMEM((near, width, width), F32),
            pltpu.VMEM((near * tiles * 8, width), F32),
            pltpu.VMEM((3, tiles, width), F32),
            pltpu.VMEM((3, near * tiles, width), F32),
            pltpu.VMEM((3, near * tiles, width), F32),
            pltpu.VMEM((3, near * tiles, width), F32),
            pltpu.VMEM((near * tiles * ROWS, width), F32),
            pltpu.VMEM((near * tiles * ROWS, width), F32),
            pltpu.VMEM(((1 + near) * tiles * ROWS, width), F32),
            vectors,
            vectors,
            vectors,
            vectors,
            pltpu.VMEM((ITERS, count, 8, width), F32),
            pltpu.SemaphoreType.DMA((2,)),
            pltpu.SemaphoreType.DMA((2, ITERS)),
            pltpu.SemaphoreType.DMA((2, ITERS)),
            pltpu.SemaphoreType.DMA((2, ITERS)),
        ],
        compiler_params=pltpu.CompilerParams(collective_id=0, has_side_effects=True),
    )(window, hits, image)
    return pl.pallas_call(
        functools.partial(untiling_kernel, tiles),
        out_shape=(out, out),
        in_specs=[vmem, vmem],
        out_specs=(vmem, vmem),
    )(found, inverse)


def solution(mesh):
    in_specs = (
        P(None, ("rep", "gx")),
        P(("rep", "gx")),
        P(None, ("rep", "gx")),
        P(("rep", "gx")),
        P(("rep", "gx"), None),
        P(None, ("rep", "gx"), None),
    )
    out_specs = (P(None, ("rep", "gx")), P(None, ("rep", "gx")))
    return jax.shard_map(
        on_device, mesh=mesh, in_specs=in_specs, out_specs=out_specs, check_vma=False
    )
```

time: 455 us -> 80.5 us (0.18)
  local copies, waits for them, and re-layouts: 143 us -> 2.24 us
  blocking collectives: 120 us -> 0 us
  other arithmetic: 104 us -> 0 us
  Pallas kernels: 0 us -> 77.4 us
  waiting for transfers between devices: 27 us -> 0 us
  loops' own time: 25.6 us -> 0 us
  between operations: 14.6 us -> 0.65 us
  starting transfers between devices: 11.7 us -> 0 us
  matrix products: 7.52 us -> 0 us
    psum x4 -> x0, blocking collectives: 120 us -> none  [two_products(): return lax.psum((jnp.sum(vector * vector), jnp.sum(vector * applied)), 'gx')]
    reduce_sum x16 -> x0, other arithmetic: 96.3 us -> none  [the longest x12 93.5 us: pair_block(): jnp.sum(lift_left * offsets[component] - coeff_three * moment_left[:, com...]
    gather x75 -> x0, local copies, waits for them, and re-layouts: 94.2 us -> none  [the longest x1 23 us: on_device(): tiled_polar = polar[tile_atom].reshape(tile_count, tile_width)]
    pallas_call x0 -> x3, Pallas kernels: none -> 77.4 us  [the longest x1 61.6 us: on_device(): pl.pallas_call(functools.partial(kernel, count, tiles, links), out_shape=...]
    ppermute x9 -> x0, waiting for transfers between devices: 27 us -> none  [passed_along(): return lax.ppermute(value, axis, pairs)]
    another operation x4 -> x0, loops' own time: 25.6 us -> none  [slab_fields(): lax.scan(accumulate, jnp.zeros((window_size, 3 * tile_width), jnp.float32...]
    scatter x2 -> x0, local copies, waits for them, and re-layouts: 22.8 us -> none  [the longest x1 11.4 us: on_device(): dipoles = jnp.zeros((3, atom_count), jnp.float32).at[:, tile_atom].set(so...]
    ppermute x9 -> x0, starting transfers between devices: 11.7 us -> none  [passed_along(): return lax.ppermute(value, axis, pairs)]
  transfers between devices with their start and end apart: 9 -> 0, of which waited for: 8 -> 0; matrix products, arithmetic and copies ran while one was open for 4% -> 0% of each run, Pallas kernels for 0% -> 0%
where the time goes in v1:
time: 80.5 us; the launch traced here: 80.3 us
  Pallas kernels  77.4 us (96%)
  local copies, waits for them, and re-layouts  2.24 us (3%)
    pallas_call x1, Pallas kernels, on_device(): pl.pallas_call(functools.partial(kernel, count, tiles, links), out_shape=...  61.6 us
    pallas_call x1, Pallas kernels, on_device(): pl.pallas_call(functools.partial(tiling_kernel, tiles, links), out_shape=...  10.6 us
    pallas_call x1, Pallas kernels, on_device(): pl.pallas_call(functools.partial(untiling_kernel, tiles), out_shape=(out,...  5.1 us

profile of v1, /device:TPU:0, one launch (start us, length us, event | category | flops | bytes accessed | tf_op | source)
XLA Modules:
  0.0 80.3 jit_solution(3628612582935114171)
XLA Ops:
  0.6 0.0 copy-start.1
  0.6 0.7 copy-done.1
  1.3 0.1 copy.9
  1.4 0.0 copy-start
  1.4 0.6 reshape.16.list_ref
  2.0 0.0 copy-done
  2.1 0.1 copy.10
  2.2 0.7 reshape.17.shift_ref
  2.9 10.6 %shard_map.77 = (f32[256,128]{1,0:T(8,128)}, s32[32,128]{1,0:T(8,128)}, f32[128,128]{1,0:T(8,128)}, f32[3,64,128]{2,1,0:T(8,128)}) custom-call(s32[96]{0:T(128)} %reshape.16.list_ref, s32[192]{0:T(256)} %reshape.17.shift_ref, f32[3,4096]{1,0:T(4,128)} %place_ref.1, f32[1,4096]{1,0:T(1,128)} %bitcast.2, f32[3,4096]{1,0:T(4,128)} %field_ref.1, s32[32,128]{1,0:T(8,128)} %bitcast.3), custom_call_target="tpu_custom_call" | custom-call | tf_op jit(solution)/shard_map/pallas_call | solution.py:505
  13.5 61.6 %shard_map.78.tiled_ref = f32[256,128]{1,0:T(8,128)} custom-call(f32[256,128]{1,0:T(8,128)} %get-tuple-element.6.tiled_ref, f32[128,128]{1,0:T(8,128)} %get-tuple-element.7.hits_ref, f32[3,64,128]{2,1,0:T(8,128)} %get-tuple-element.8.image_ref), custom_call_target="tpu_custom_call" | custom-call | tf_op jit(solution)/shard_map/pallas_call | solution.py:524
  75.2 5.1 %shard_map.79 = (f32[3,4096]{1,0:T(4,128)}, f32[3,4096]{1,0:T(4,128)}) custom-call(f32[256,128]{1,0:T(8,128)} %shard_map.78.tiled_ref, s32[32,128]{1,0:T(8,128)} %get-tuple-element.9.inverse), custom_call_target="tpu_custom_call" | custom-call | tf_op jit(solution)/shard_map/pallas_call | solution.py:556
Async XLA Ops:
  0.6 0.7 copy-start.1
  1.4 0.7 copy-start

commit v2 on v1

--- a/solution.py
+++ b/solution.py
@@ -72,7 +72,7 @@
         out_ref[pl.ds(pl.multiple_of(tile * 8, 8), 8), :] = value
         return carry
 
-    lax.fori_loop(0, tiles, fill, 0)
+    lax.fori_loop(0, tiles, fill, 0, unroll=4)
 
     lane_ids = lax.broadcasted_iota(jnp.int32, (width, width), 0)
     tile_ids = lax.broadcasted_iota(jnp.int32, (tiles, width), 0)
@@ -90,7 +90,9 @@
             left, right, (((1,), (1,)), ((), ())), preferred_element_type=F32
         )
 
-    found = lax.fori_loop(0, tiles, invert, jnp.zeros((2 * tiles, width), F32))
+    found = lax.fori_loop(
+        0, tiles, invert, jnp.zeros((2 * tiles, width), F32), unroll=4
+    )
     inverse[...] = (found[:tiles] * float(width) + found[tiles:]).astype(jnp.int32)
 
     lane_one = lax.broadcasted_iota(jnp.int32, (1, width), 1)
@@ -111,7 +113,7 @@
             image[2, pl.ds(slot, 1), :] = ones * step_z
         return carry
 
-    lax.fori_loop(0, tiles, name, 0)
+    lax.fori_loop(0, tiles, name, 0, unroll=4)
 
 
 def untiling_kernel(tiles, tiled_ref, inverse, dip_ref, res_ref):
@@ -124,7 +126,7 @@
         res_ref[:, lanes] = value[3:6]
         return carry
 
-    lax.fori_loop(0, tiles, give, 0)
+    lax.fori_loop(0, tiles, give, 0, unroll=4)
 
 
 def kernel(

time: 80.5 us -> 73.4 us (0.912)
  Pallas kernels: 77.4 us -> 70.3 us
    pallas_call x1, Pallas kernels: 10.6 us -> 5.32 us  [on_device(): pl.pallas_call(functools.partial(tiling_kernel, tiles, links), out_shape=...]
    pallas_call x1, Pallas kernels: 5.1 us -> 3.32 us  [on_device(): pl.pallas_call(functools.partial(untiling_kernel, tiles), out_shape=(out,...]
where the time goes in v2:
time: 73.4 us; the launch traced here: 73.2 us
  Pallas kernels  70.3 us (96%)
  local copies, waits for them, and re-layouts  2.24 us (3%)
    pallas_call x1, Pallas kernels, on_device(): pl.pallas_call(functools.partial(kernel, count, tiles, links), out_shape=...  61.6 us
    pallas_call x1, Pallas kernels, on_device(): pl.pallas_call(functools.partial(tiling_kernel, tiles, links), out_shape=...  5.32 us
    pallas_call x1, Pallas kernels, on_device(): pl.pallas_call(functools.partial(untiling_kernel, tiles), out_shape=(out,...  3.32 us

profile of v2, /device:TPU:0, one launch (start us, length us, event | category | flops | bytes accessed | tf_op | source)
XLA Modules:
  0.0 73.2 jit_solution(9993016525571853515)
XLA Ops:
  0.6 0.0 copy-start.1
  0.6 0.7 copy-done.1
  1.3 0.1 copy.9
  1.4 0.0 copy-start
  1.4 0.6 reshape.16.list_ref
  2.0 0.0 copy-done
  2.1 0.1 copy.10
  2.2 0.7 reshape.17.shift_ref
  2.9 5.3 %shard_map.77 = (f32[256,128]{1,0:T(8,128)}, s32[32,128]{1,0:T(8,128)}, f32[128,128]{1,0:T(8,128)}, f32[3,64,128]{2,1,0:T(8,128)}) custom-call(s32[96]{0:T(128)} %reshape.16.list_ref, s32[192]{0:T(256)} %reshape.17.shift_ref, f32[3,4096]{1,0:T(4,128)} %place_ref.1, f32[1,4096]{1,0:T(1,128)} %bitcast.2, f32[3,4096]{1,0:T(4,128)} %field_ref.1, s32[32,128]{1,0:T(8,128)} %bitcast.3), custom_call_target="tpu_custom_call" | custom-call | tf_op jit(solution)/shard_map/pallas_call | solution.py:507
  8.2 61.6 %shard_map.78.tiled_ref = f32[256,128]{1,0:T(8,128)} custom-call(f32[256,128]{1,0:T(8,128)} %get-tuple-element.6.tiled_ref, f32[128,128]{1,0:T(8,128)} %get-tuple-element.7.hits_ref, f32[3,64,128]{2,1,0:T(8,128)} %get-tuple-element.8.image_ref), custom_call_target="tpu_custom_call" | custom-call | tf_op jit(solution)/shard_map/pallas_call | solution.py:526
  69.8 3.3 %shard_map.79 = (f32[3,4096]{1,0:T(4,128)}, f32[3,4096]{1,0:T(4,128)}) custom-call(f32[256,128]{1,0:T(8,128)} %shard_map.78.tiled_ref, s32[32,128]{1,0:T(8,128)} %get-tuple-element.9.inverse), custom_call_target="tpu_custom_call" | custom-call | tf_op jit(solution)/shard_map/pallas_call | solution.py:558
Async XLA Ops:
  0.6 0.7 copy-start.1
  1.4 0.7 copy-start
